TPU v7x, 512 devices: a whole 4x8x8 slice. The times are simulated.
512 devices in a mesh: rows: 32 (over z, x), tp: 2 (over core), job: 8 (over y).
Axes of the slice: x: 4, y: 8, z: 8, core: 2. Of those that a mesh axis runs over, the one named last changes fastest.
Arguments:
- train_query: bfloat16 [16384, 2048], P(('job', 'rows'), 'tp'), parts along dimension 0, may hold values from -0.125 to 0.125
- low_query: bfloat16 [16384, 16], P(('job', 'rows')), parts along dimension 0, may hold values from -0.125 to 0.125
- high_query: bfloat16 [128, 2048], P('job', 'tp'), parts along dimension 0, may hold values from -1.5 to 1.5
- train_key: bfloat16 [16384, 512], P(('job', 'rows'), 'tp'), parts along dimension 0, may hold values from -0.125 to 0.125
- low_key: bfloat16 [16384, 16], P(('job', 'rows')), parts along dimension 0, may hold values from -0.125 to 0.125
- high_key: bfloat16 [128, 512], P('job', 'tp'), parts along dimension 0, may hold values from -1.5 to 1.5
- train_value: bfloat16 [16384, 512], P(('job', 'rows'), 'tp'), parts along dimension 0, may hold values from -0.125 to 0.125
- low_value: bfloat16 [16384, 16], P(('job', 'rows')), parts along dimension 0, may hold values from -0.125 to 0.125
- high_value: bfloat16 [128, 512], P('job', 'tp'), parts along dimension 0, may hold values from -1.5 to 1.5
- norm_train: float32 [16384], P(('job', 'rows', 'tp')), parts along dimension 0, may hold values from 0.25 to 1.75
- norm_step: float32 [16384], P(('job', 'rows', 'tp')), parts along dimension 0, may hold values from -0.3 to 0.3
Outputs:
- serve_query: bfloat16 [16384, 2048], P(('job', 'tp')), parts along dimension 0
- serve_key: bfloat16 [4096, 2048], P(('job', 'tp')), parts along dimension 0
- serve_value: bfloat16 [4096, 2048], P(('job', 'tp')), parts along dimension 0
- serve_norm: bfloat16 [16384], P('job'), parts along dimension 0
There are 8 independent parts, one for each index of `job`. A program takes and returns all parts, laid end to end along the dimension named above; each array names one. Nothing has to cross between parts.
All inputs are finite; a program needn't handle non-finite values.
Results may differ from a plain program's by a relative error of at most 0.001.
Values may be sent and summed in bfloat16 or wider, within the bound.
A program may use at most 64 MiB of HBM per device.

v0:
```python
import jax
import jax.numpy as jnp
from jax import lax
from jax.sharding import PartitionSpec as P

mix_rate = 0.5


def in_one_piece(arrays, axis, dim, along):
    widths = [a.shape[along] for a in arrays]
    both = jnp.concatenate(arrays, axis=along)
    out = lax.all_gather(both, axis, axis=dim, tiled=True)
    return tuple(jnp.split(out, [sum(widths[:k]) for k in range(1, len(widths))], axis=along))


def in_order(pieces, dim):
    pieces = jnp.moveaxis(pieces, 0, dim)
    lengths = pieces.shape
    return pieces.reshape(*lengths[:dim], lengths[dim] * lengths[dim + 1], *lengths[dim + 2 :])


def from_everyone(shard, axis):
    length = lax.axis_size(axis)
    return lax.all_to_all(
        jnp.broadcast_to(shard[None], (length, *shard.shape)), axis, 0, 0, tiled=True
    )


def gathered_copies(shard, axis, dim):
    return in_order(from_everyone(shard, axis), dim)


def local(
    train_query,
    low_query,
    high_query,
    train_key,
    low_key,
    high_key,
    train_value,
    low_value,
    high_value,
    norm_train,
    norm_step,
):
    fresh_query = train_query.astype(jnp.float32) + mix_rate * jnp.dot(
        low_query, high_query, preferred_element_type=jnp.float32
    )
    fresh_key = train_key.astype(jnp.float32) + mix_rate * jnp.dot(
        low_key, high_key, preferred_element_type=jnp.float32
    )
    fresh_value = train_value.astype(jnp.float32) + mix_rate * jnp.dot(
        low_value, high_value, preferred_element_type=jnp.float32
    )
    narrow_query, narrow_key, narrow_value = (
        fresh_query.astype(jnp.bfloat16),
        fresh_key.astype(jnp.bfloat16),
        fresh_value.astype(jnp.bfloat16),
    )
    serve_query, serve_key, serve_value = in_one_piece(
        (narrow_query, narrow_key, narrow_value), "rows", 0, 1
    )
    serve_query, serve_key, serve_value = (serve_query.T, serve_key.T, serve_value.T)
    serve_norm = gathered_copies((norm_train + norm_step).astype(jnp.bfloat16), ("rows", "tp"), 0)
    return (serve_query, serve_key, serve_value, serve_norm)


def solution(mesh):
    in_specs = (
        P(("job", "rows"), "tp"),
        P(("job", "rows"), None),
        P("job", "tp"),
        P(("job", "rows"), "tp"),
        P(("job", "rows"), None),
        P("job", "tp"),
        P(("job", "rows"), "tp"),
        P(("job", "rows"), None),
        P("job", "tp"),
        P(("job", "rows", "tp")),
        P(("job", "rows", "tp")),
    )
    out_specs = (P(("job", "tp"), None), P(("job", "tp"), None), P(("job", "tp"), None), P("job"))
    return jax.shard_map(local, mesh=mesh, in_specs=in_specs, out_specs=out_specs, check_vma=False)
```

profile of v0, /device:TPU:56, one launch (start us, length us, event | category | flops | bytes accessed | tf_op | source)
XLA Modules:
  0.0 132.6 jit_solution(12054167524016155888)
XLA Ops:
  7.2 0.0 copy-start
  7.2 0.0 all-gather.2.cloned.1.call-start
  7.2 0.7 copy-done
  7.9 1.1 fusion.1
  9.1 1.0 fusion.4
  10.0 1.0 fusion.5
  11.0 0.7 pad_maximum_fusion
  11.7 0.0 all-gather.2.cloned.1.call-update
  11.7 0.7 add_convert_fusion
  12.4 23.2 %all_to_all.6 = bf16[64,1,32]{2,1,0:T(2,128)(2,1)S(1)} all-to-all(bf16[64,1,32]{2,1,0:T(2,128)(2,1)S(1)} %broadcast_in_dim.2), channel_id=1, replica_groups=mesh['rows'=32,'tp'=2,'job'=8] {'rows','tp'}, dimensions={0} | all-to-all | bytes 8192 | tf_op jit(solution)/shard_map/all_to_all | solution.py:24
  35.7 0.1 reduce
  35.8 0.7 reshape.18
  36.4 73.7 %all-gather.2.cloned.1.call-done = bf16[2048,1536]{1,0:T(8,128)(2,1)} async-done(((bf16[64,1536]{1,0:T(8,128)(2,1)}), bf16[2048,1536]{1,0:T(8,128)(2,1)}) %all-gather.2.cloned.1.call-update) | async-done | bytes 6291472 | tf_op jit(solution)/shard_map/all_gather | solution.py:12
  110.2 1.7 %slice_bitcast_fusion.1 = (bf16[256,2048]{0,1:T(8,128)(2,1)S(1)}, bf16[256,2048]{0,1:T(8,128)(2,1)S(1)}) fusion(bf16[2048,1536]{1,0:T(8,128)(2,1)} %all-gather.2.cloned.1.call-done), kind=kLoop, calls=%fused_computation.10 | loop fusion | bytes 4194304 | tf_op jit(solution)/shard_map/transpose | solution.py:63
  111.9 1.4 %copy.22 = bf16[256,2048]{1,0:T(8,128)(2,1)} copy(bf16[256,2048]{0,1:T(8,128)(2,1)S(1)} %get-tuple-element.17) | data formatting | bytes 2097152
  113.3 1.4 %copy.23 = bf16[256,2048]{1,0:T(8,128)(2,1)} copy(bf16[256,2048]{0,1:T(8,128)(2,1)S(1)} %get-tuple-element.16) | data formatting | bytes 2097152
  114.7 4.6 %slice_bitcast_fusion = bf16[1024,2048]{0,1:T(8,128)(2,1)} fusion(bf16[2048,1536]{1,0:T(8,128)(2,1)} %all-gather.2.cloned.1.call-done), kind=kLoop, calls=%fused_computation | loop fusion | bytes 8388608 | tf_op jit(solution)/shard_map/transpose | solution.py:63
  119.4 6.4 %copy.21 = bf16[1024,2048]{1,0:T(8,128)(2,1)} copy(bf16[1024,2048]{0,1:T(8,128)(2,1)} %slice_bitcast_fusion) | data formatting | bytes 8388608
  (1 shorter events, 0.0 us)
Async XLA Ops:
  7.2 0.8 copy-start
  7.2 103.0 %all-gather.2.cloned.1.call-start = ((), (), s32[]{:S(2)}) async-start(), calls=%async_computation.1 | async-start | bytes 6488064 | tf_op jit(solution)/shard_map/all_gather | solution.py:12
Sparse Core Ops, SparseCore 0:
  11.9 98.2 all-gather.1
where the time goes:
time: 134 us; the launch traced here: 133 us
  waiting for transfers between devices  73.8 us (55%)
  blocking collectives  23.2 us (17%)
  local copies, waits for them, and re-layouts  17 us (13%)
  between operations  14.1 us (11%)
  matrix products  3.07 us (2%)
  other arithmetic  1.47 us (1%)
    all_gather x1, waiting for transfers between devices, in_one_piece(): out = lax.all_gather(both, axis, axis=dim, tiled=True)  73.7 us
    all_to_all x1, blocking collectives, from_everyone(): lax.all_to_all(jnp.broadcast_to(shard[None], (length, *shard.shape)), axi...  23.2 us
    unnamed x5, local copies, waits for them, and re-layouts  9.97 us
    transpose x2, local copies, waits for them, and re-layouts, local(): serve_query, serve_key, serve_value = (serve_query.T, serve_key.T, serve_...  6.34 us
  transfers between devices with their start and end apart: 1, of which 1 were waited for; matrix products, arithmetic and copies ran while one was open for 1% of the time, Pallas kernels for 0%

commit v1 on v0

v1 whole, which is shorter than its diff:
```python
import functools
import heapq
import itertools

import jax
import jax.numpy as jnp
from jax import lax
from jax.experimental import pallas as pl
from jax.experimental.pallas import tpu as pltpu
from jax.sharding import PartitionSpec as P

MESH = pl.DeviceIdType.MESH
mix_rate = 0.5

Z, X = 8, 4
RATE = 46650.0
HOP = 2.0
DEPTH = 2

PIECES = (("x", 640, 1), ("z", 512, 1), ("z", 384, -1))
FIRST = (1, 0, 2)


def onward(d, size, far):
    if d == 0:
        return [(1, 1), (-1, -1)]
    side = 1 if d > 0 else -1
    limit = size // 2 if side == far else size // 2 - 1
    return [(d + side, side)] if abs(d) < limit else []


def forwards(item):
    kind, dx, dz = item
    out = []
    if kind == "sum_x":
        return [("x", s, ("sum_x", n, 0)) for n, s in onward(dx, X, 1)]
    if kind == "sum_z":
        return [("z", s, ("sum_z", 0, n)) for n, s in onward(dz, Z, 1)]
    axis, _, far = PIECES[kind]
    if axis == "x":
        if dz == 0:
            out += [("x", s, (kind, n, 0)) for n, s in onward(dx, X, far)]
        out += [("z", s, (kind, dx, n)) for n, s in onward(dz, Z, 1 if dx % 2 == 0 else -1)]
    else:
        if dx == 0:
            out += [("z", s, (kind, 0, n)) for n, s in onward(dz, Z, far)]
        out += [("x", s, (kind, n, dz)) for n, s in onward(dx, X, 1 if dz % 2 == 0 else -1)]
    return out


def left_to_go(item):
    after = forwards(item)
    return 1 + max(left_to_go(n) for _, _, n in after) if after else 0


def plan():
    links = {(a, s): [] for a in "xz" for s in (1, -1)}
    given = {k: [] for k in links}
    events, tick, steps = [], itertools.count(), []
    norm_x, norm_z = 1, 1

    def cost(item):
        return (512 if isinstance(item[0], str) else PIECES[item[0]][1] * 128) / RATE

    def offer(item):
        for axis, side, there in forwards(item):
            rank = -1000 if isinstance(item[0], str) else -left_to_go(there)
            links[axis, side].append((rank, next(tick), item, there))

    def begin(k, now):
        item = given[k][0]
        heapq.heappush(events, (now + cost(item), next(tick), "done", k, item))

    def feed(now):
        for k in links:
            while links[k] and len(given[k]) < DEPTH:
                links[k].sort()
                _, _, item, there = links[k].pop(0)
                steps.append(("send", k[0], k[1], item, there))
                given[k].append(there)
                if len(given[k]) == 1:
                    begin(k, now)

    offer(("sum_x", 0, 0))
    for kind in FIRST:
        offer((kind, 0, 0))
    feed(0.0)
    while events:
        now, _, what, k, item = heapq.heappop(events)
        if what == "done":
            given[k].pop(0)
            if given[k]:
                begin(k, now)
            heapq.heappush(events, (now + HOP, next(tick), "here", k, item))
            feed(now)
            continue
        steps.append(("wait", item))
        if item[0] == "sum_x":
            norm_x += 1
            if norm_x == X:
                offer(("sum_z", 0, 0))
        elif item[0] == "sum_z":
            norm_z += 1
        offer(item)
        feed(now)
        if item[0] == "sum_z" and norm_z == Z:
            steps.append(("swap",))
    return steps


def kernel(
    steps, places, tq, lq, hq, tk, lk, hk, tv, lv, hv, nt, ns, oq, ok, ov, on, *scratch
):
    vin, blocks, sums = scratch[:11], scratch[11 : 11 + len(PIECES)], scratch[11 + len(PIECES)]
    in_sem, send_sem, recv_sem, swap_sem = scratch[12 + len(PIECES) :]
    me, tp = lax.axis_index("rows"), lax.axis_index("tp")
    mz, mx = me // X, me % X

    def row(dx, dz):
        return ((mz - dz + Z) % Z) * X + (mx - dx + X) % X

    loads = [
        pltpu.make_async_copy(a, b, in_sem.at[i])
        for i, (a, b) in enumerate(zip((tq, lq, hq, tk, lk, hk, tv, lv, hv, nt, ns), vin))
    ]
    for load in loads:
        load.start()

    barrier = pltpu.get_barrier_semaphore()
    for there in (row(1, 0), row(-1, 0), row(0, 1), row(0, -1)):
        pl.semaphore_signal(barrier, inc=1, device_id={"rows": there}, device_id_type=MESH)
    pl.semaphore_signal(barrier, inc=1, device_id={"tp": 1 - tp}, device_id_type=MESH)

    for load in loads:
        load.wait()
    vtq, vlq, vhq, vtk, vlk, vhk, vtv, vlv, vhv, vnt, vns = vin

    def merged(train, low, high, lo, hi):
        product = lax.dot_general(
            low[...], high[:, lo:hi], (((0,), (0,)), ((), ())), preferred_element_type=jnp.float32
        )
        return (train[:, lo:hi].astype(jnp.float32) + mix_rate * product).astype(jnp.bfloat16)

    cut = PIECES[0][1]
    width = vtq.shape[1]
    kv = vtk.shape[1]
    sums[tp, me] = jnp.concatenate(
        [vnt[...] + vns[...], jnp.zeros((1, 128 - vnt.shape[1]), jnp.float32)], axis=1
    )
    blocks[1][me, :, :kv] = merged(vtk, vlk, vhk, 0, kv)
    blocks[1][me, :, kv:] = merged(vtv, vlv, vhv, 0, kv)
    blocks[0][me] = merged(vtq, vlq, vhq, 0, cut)
    blocks[2][me] = merged(vtq, vlq, vhq, cut, width)
    pl.semaphore_wait(barrier, 5)

    def copy(axis, side, item, there):
        kind, dx, dz = item
        if kind == "sum_x":
            ref = sums.at[tp, row(dx, 0)]
        elif kind == "sum_z":
            ref = sums.at[tp, pl.ds(((mz - dz + Z) % Z) * X, X)]
        else:
            ref = blocks[kind].at[row(dx, dz)]
        target = row(-side, 0) if axis == "x" else row(0, -side)
        n = places[there]
        return pltpu.make_async_remote_copy(
            src_ref=ref,
            dst_ref=ref,
            send_sem=send_sem.at[n],
            recv_sem=recv_sem.at[n],
            device_id={"rows": target},
            device_id_type=MESH,
        )

    def landed(item):
        kind, dx, dz = item
        if kind == "sum_x":
            ref = sums.at[tp, row(dx, 0)]
        elif kind == "sum_z":
            ref = sums.at[tp, pl.ds(((mz - dz + Z) % Z) * X, X)]
        else:
            ref = blocks[kind].at[row(dx, dz)]
        n = places[item]
        return pltpu.make_async_remote_copy(
            src_ref=ref,
            dst_ref=ref,
            send_sem=send_sem.at[n],
            recv_sem=recv_sem.at[n],
            device_id={"rows": row(1, 0)},
            device_id_type=MESH,
        )

    def turn(kind, pair):
        both = blocks[kind][pl.ds(pair * 2, 2)]
        rows, columns = both.shape[1], both.shape[2]
        lanes = pl.ds(pl.multiple_of(pair * 2 * rows, 2 * rows), 2 * rows)
        flat = both.reshape(2 * rows, columns)
        if kind == 0:
            oq[:columns, lanes] = flat.T
        elif kind == 1:
            ok[:, lanes] = flat[:, :kv].T
            ov[:, lanes] = flat[:, kv:].T
        else:
            oq[cut:, lanes] = flat.T

    sent, swap = [], None
    here = {(kind, dz): {0} if dz == 0 else set() for kind in range(len(PIECES)) for dz in range(Z)}
    for step in steps:
        if step[0] == "send":
            c = copy(*step[1:])
            c.start()
            sent.append(c)
        elif step[0] == "swap":
            swap = pltpu.make_async_remote_copy(
                src_ref=sums.at[tp],
                dst_ref=sums.at[tp],
                send_sem=swap_sem.at[0],
                recv_sem=swap_sem.at[1],
                device_id={"tp": 1 - tp},
                device_id_type=MESH,
            )
            swap.start()
        else:
            item = step[1]
            landed(item).wait_recv()
            kind, dx, dz = item
            if isinstance(kind, str):
                continue
            got = here[kind, dz % Z]
            before = {0, 1, 3} <= got, len(got) == X
            got.add(dx % X)
            after = {0, 1, 3} <= got, len(got) == X
            zz = (mz - dz + Z) % Z
            if after[0] and not before[0]:
                turn(kind, zz * 2 + mx // 2)
            if after[1] and not before[1]:
                turn(kind, zz * 2 + 1 - mx // 2)
    swap.wait()
    g = [sums[i].reshape(Z * X // 2, 2, 128) for i in range(2)]
    parts = [g[j % 2][:, j // 2] for j in range(4)]
    total = parts[0]
    for j in range(1, 4):
        total = total + pltpu.roll(parts[j], 32 * j, axis=1)
    on[...] = total.astype(jnp.bfloat16)
    for c in sent:
        c.wait_send()


def local(tq, lq, hq, tk, lk, hk, tv, lv, hv, nt, ns):
    steps = plan()
    places = {s[4]: i for i, s in enumerate(s for s in steps if s[0] == "send")}
    rows, wide = tq.shape
    kv = tk.shape[1]
    n = Z * X
    args = (tq, lq.T, hq, tk, lk.T, hk, tv, lv.T, hv, nt.reshape(1, -1), ns.reshape(1, -1))
    args = tuple(pltpu.with_memory_space_constraint(a, pltpu.HBM) for a in args)
    q, k, v, norm = pl.pallas_call(
        functools.partial(kernel, steps, places),
        name="gather",
        out_shape=(
            jax.ShapeDtypeStruct((wide, n * rows), jnp.bfloat16),
            jax.ShapeDtypeStruct((kv, n * rows), jnp.bfloat16),
            jax.ShapeDtypeStruct((kv, n * rows), jnp.bfloat16),
            jax.ShapeDtypeStruct((n // 2, 128), jnp.bfloat16),
        ),
        in_specs=[pl.BlockSpec(memory_space=pltpu.HBM)] * 11,
        out_specs=(pl.BlockSpec(memory_space=pltpu.VMEM),) * 4,
        scratch_shapes=[
            *(pltpu.VMEM(a.shape, a.dtype) for a in args),
            *(pltpu.VMEM((n, rows, columns), jnp.bfloat16) for _, columns, _ in PIECES),
            pltpu.VMEM((2, n, 1, 128), jnp.float32),
            pltpu.SemaphoreType.DMA((11,)),
            pltpu.SemaphoreType.DMA((len(places),)),
            pltpu.SemaphoreType.DMA((len(places),)),
            pltpu.SemaphoreType.DMA((2,)),
        ],
        compiler_params=pltpu.CompilerParams(
            collective_id=0, has_side_effects=True, vmem_limit_bytes=24 * 1024 * 1024
        ),
    )(*args)
    return q, k, v, norm.reshape(-1)


def solution(mesh):
    in_specs = (
        P(("job", "rows"), "tp"),
        P(("job", "rows"), None),
        P("job", "tp"),
        P(("job", "rows"), "tp"),
        P(("job", "rows"), None),
        P("job", "tp"),
        P(("job", "rows"), "tp"),
        P(("job", "rows"), None),
        P("job", "tp"),
        P(("job", "rows", "tp")),
        P(("job", "rows", "tp")),
    )
    out_specs = (P(("job", "tp"), None), P(("job", "tp"), None), P(("job", "tp"), None), P("job"))
    return jax.shard_map(local, mesh=mesh, in_specs=in_specs, out_specs=out_specs, check_vma=False)
```

time: 134 us -> 55.9 us (0.42)
  waiting for transfers between devices: 73.8 us -> 0 us
  Pallas kernels: 0 us -> 50.6 us
  blocking collectives: 23.2 us -> 0 us
  between operations: 14.1 us -> 0.64 us
  local copies, waits for them, and re-layouts: 17 us -> 4.55 us
  matrix products: 3.07 us -> 0 us
  other arithmetic: 1.47 us -> 0 us
    all_gather x1 -> x0, waiting for transfers between devices: 73.7 us -> none  [in_one_piece(): out = lax.all_gather(both, axis, axis=dim, tiled=True)]
    pallas_call x0 -> x1, Pallas kernels: none -> 50.6 us  [local(): pl.pallas_call(functools.partial(kernel, steps, places), name='gather', o...]
    all_to_all x1 -> x0, blocking collectives: 23.2 us -> none  [from_everyone(): lax.all_to_all(jnp.broadcast_to(shard[None], (length, *shard.shape)), axi...]
    transpose x2 -> x0, local copies, waits for them, and re-layouts: 6.34 us -> none  [local(): serve_query, serve_key, serve_value = (serve_query.T, serve_key.T, serve_...]
    unnamed x5 -> x4, local copies, waits for them, and re-layouts: 9.97 us -> 4.55 us
    dot_general x3 -> x0, matrix products: 3.07 us -> none  [the longest x1 1.13 us: local(): jnp.dot(low_query, high_query, preferred_element_type=jnp.float32)]
  transfers between devices with their start and end apart: 1 -> 0, of which waited for: 1 -> 0; matrix products, arithmetic and copies ran while one was open for 1% -> 0% of each run, Pallas kernels for 0% -> 0%
where the time goes in v1:
time: 55.9 us; the launch traced here: 55.8 us
  Pallas kernels  50.6 us (91%)
  local copies, waits for them, and re-layouts  4.55 us (8%)
  between operations  0.64 us (1%)
    pallas_call x1, Pallas kernels, local(): pl.pallas_call(functools.partial(kernel, steps, places), name='gather', o...  50.6 us
    unnamed x4, local copies, waits for them, and re-layouts  4.55 us

profile of v1, /device:TPU:56, one launch (start us, length us, event | category | flops | bytes accessed | tf_op | source)
XLA Modules:
  0.0 55.8 jit_solution(10274952677380420335)
XLA Ops:
  0.6 50.6 %gather.1 = (bf16[1024,2048]{1,0:T(8,128)(2,1)S(1)}, bf16[256,2048]{1,0:T(8,128)(2,1)S(1)}, bf16[256,2048]{1,0:T(8,128)(2,1)S(1)}, bf16[16,128]{1,0:T(8,128)(2,1)S(1)}) custom-call(bf16[64,1024]{1,0:T(8,128)(2,1)} %tq.1, bf16[16,64]{1,0:T(8,128)(2,1)} %bitcast.7, bf16[16,1024]{1,0:T(8,128)(2,1)} %hq.1, bf16[64,256]{1,0:T(8,128)(2,1)} %tk.1, ...), custom_call_target="tpu_custom_call" | custom-call | tf_op jit(solution)/shard_map/gather/pallas_call | solution.py:257
  51.2 2.0 %copy.19 = bf16[1024,2048]{1,0:T(8,128)(2,1)} copy(bf16[1024,2048]{1,0:T(8,128)(2,1)S(1)} %get-tuple-element.16) | data formatting | bytes 8388608
  53.3 1.0 %copy.20 = bf16[256,2048]{1,0:T(8,128)(2,1)} copy(bf16[256,2048]{1,0:T(8,128)(2,1)S(1)} %get-tuple-element.17) | data formatting | bytes 2097152
  54.2 1.0 %copy.21 = bf16[256,2048]{1,0:T(8,128)(2,1)} copy(bf16[256,2048]{1,0:T(8,128)(2,1)S(1)} %get-tuple-element.18) | data formatting | bytes 2097152
  55.2 0.6 %copy.22 = bf16[2048]{0:T(1024)(128)(2,1)} copy(bf16[2048]{0:T(1024)(128)(2,1)S(1)} %bitcast.6) | data formatting | bytes 8192

commit v2 on v1

--- a/solution.py
+++ b/solution.py
@@ -246,6 +246,16 @@
         c.wait_send()
 
 
+def write_out(*refs):
+    n = len(refs) // 2
+    sem = refs[-1]
+    copies = [pltpu.make_async_copy(refs[i], refs[n + i], sem.at[i]) for i in range(n)]
+    for c in copies:
+        c.start()
+    for c in copies:
+        c.wait()
+
+
 def local(tq, lq, hq, tk, lk, hk, tv, lv, hv, nt, ns):
     steps = plan()
     places = {s[4]: i for i, s in enumerate(s for s in steps if s[0] == "send")}
@@ -278,6 +288,16 @@
             collective_id=0, has_side_effects=True, vmem_limit_bytes=24 * 1024 * 1024
         ),
     )(*args)
+    held = tuple(pltpu.with_memory_space_constraint(a, pltpu.VMEM) for a in (q, k, v, norm))
+    q, k, v, norm = pl.pallas_call(
+        write_out,
+        name="write",
+        out_shape=tuple(jax.ShapeDtypeStruct(a.shape, a.dtype) for a in held),
+        in_specs=[pl.BlockSpec(memory_space=pltpu.VMEM)] * 4,
+        out_specs=(pl.BlockSpec(memory_space=pltpu.HBM),) * 4,
+        scratch_shapes=[pltpu.SemaphoreType.DMA((4,))],
+        compiler_params=pltpu.CompilerParams(vmem_limit_bytes=1024 * 1024),
+    )(*held)
     return q, k, v, norm.reshape(-1)
 
 

time: 55.9 us -> 54.1 us (0.968)
  local copies, waits for them, and re-layouts: 4.55 us -> 0 us
  Pallas kernels: 50.6 us -> 53.3 us
    unnamed x4 -> x0, local copies, waits for them, and re-layouts: 4.55 us -> none
    pallas_call x0 -> x1, Pallas kernels: none -> 2.71 us  [local(): pl.pallas_call(write_out, name='write', out_shape=tuple((jax.ShapeDtypeSt...]
where the time goes in v2:
time: 54.1 us; the launch traced here: 54 us
  Pallas kernels  53.3 us (99%)
  between operations  0.64 us (1%)
    pallas_call x1, Pallas kernels, local(): pl.pallas_call(functools.partial(kernel, steps, places), name='gather', o...  50.6 us
    pallas_call x1, Pallas kernels, local(): pl.pallas_call(write_out, name='write', out_shape=tuple((jax.ShapeDtypeSt...  2.71 us

profile of v2, /device:TPU:56, one launch (start us, length us, event | category | flops | bytes accessed | tf_op | source)
XLA Modules:
  0.0 54.0 jit_solution(953849179936204460)
XLA Ops:
  0.6 50.6 %gather.1 = (bf16[1024,2048]{1,0:T(8,128)(2,1)S(1)}, bf16[256,2048]{1,0:T(8,128)(2,1)S(1)}, bf16[256,2048]{1,0:T(8,128)(2,1)S(1)}, bf16[16,128]{1,0:T(8,128)(2,1)S(1)}) custom-call(bf16[64,1024]{1,0:T(8,128)(2,1)} %tq.1, bf16[16,64]{1,0:T(8,128)(2,1)} %bitcast.6, bf16[16,1024]{1,0:T(8,128)(2,1)} %hq.1, bf16[64,256]{1,0:T(8,128)(2,1)} %tk.1, ...), custom_call_target="tpu_custom_call" | custom-call | tf_op jit(solution)/shard_map/gather/pallas_call | solution.py:267
  51.2 2.7 %write.1 = (bf16[1024,2048]{1,0:T(8,128)(2,1)}, bf16[256,2048]{1,0:T(8,128)(2,1)}, bf16[256,2048]{1,0:T(8,128)(2,1)}, bf16[16,128]{1,0:T(8,128)(2,1)}) custom-call(bf16[1024,2048]{1,0:T(8,128)(2,1)S(1)} %get-tuple-element.12.refs_0_, bf16[256,2048]{1,0:T(8,128)(2,1)S(1)} %get-tuple-element.13.refs_1_, bf16[256,2048]{1,0:T(8,128)(2,1)S(1)} %get-tuple-element.14.refs_2_, ...), custom_call_target="tpu_custom_call" | custom-call | tf_op jit(solution)/shard_map/write/pallas_call | solution.py:292

commit v3 on v2

--- a/solution.py
+++ b/solution.py
@@ -119,19 +119,18 @@
     def row(dx, dz):
         return ((mz - dz + Z) % Z) * X + (mx - dx + X) % X
 
+    barrier = pltpu.get_barrier_semaphore()
+    for there in (row(1, 0), row(-1, 0), row(0, 1), row(0, -1)):
+        pl.semaphore_signal(barrier, inc=1, device_id={"rows": there}, device_id_type=MESH)
+    pl.semaphore_signal(barrier, inc=1, device_id={"tp": 1 - tp}, device_id_type=MESH)
+
     loads = [
         pltpu.make_async_copy(a, b, in_sem.at[i])
         for i, (a, b) in enumerate(zip((tq, lq, hq, tk, lk, hk, tv, lv, hv, nt, ns), vin))
     ]
-    for load in loads:
+    for load in loads[3:] + loads[:3]:
         load.start()
-
-    barrier = pltpu.get_barrier_semaphore()
-    for there in (row(1, 0), row(-1, 0), row(0, 1), row(0, -1)):
-        pl.semaphore_signal(barrier, inc=1, device_id={"rows": there}, device_id_type=MESH)
-    pl.semaphore_signal(barrier, inc=1, device_id={"tp": 1 - tp}, device_id_type=MESH)
-
-    for load in loads:
+    for load in loads[3:]:
         load.wait()
     vtq, vlq, vhq, vtk, vlk, vhk, vtv, vlv, vhv, vnt, vns = vin
 
@@ -149,9 +148,33 @@
     )
     blocks[1][me, :, :kv] = merged(vtk, vlk, vhk, 0, kv)
     blocks[1][me, :, kv:] = merged(vtv, vlv, vhv, 0, kv)
-    blocks[0][me] = merged(vtq, vlq, vhq, 0, cut)
-    blocks[2][me] = merged(vtq, vlq, vhq, cut, width)
     pl.semaphore_wait(barrier, 5)
+
+    def merge_query():
+        for load in loads[:3]:
+            load.wait()
+        blocks[0][me] = merged(vtq, vlq, vhq, 0, cut)
+        blocks[2][me] = merged(vtq, vlq, vhq, cut, width)
+
+    def send_sem_of(kind):
+        return send_sem.at[("sum_x", "sum_z").index(kind) + len(PIECES) if isinstance(kind, str) else kind]
+
+    def all_sent(kind):
+        count = Z * X - 1
+        if kind == "sum_x":
+            ref = sums.at[tp, pl.ds(0, X - 1)]
+        elif kind == "sum_z":
+            ref = sums.at[tp, pl.ds(0, (Z - 1) * X)]
+        else:
+            ref = blocks[kind].at[pl.ds(0, count)]
+        pltpu.make_async_remote_copy(
+            src_ref=ref,
+            dst_ref=ref,
+            send_sem=send_sem_of(kind),
+            recv_sem=recv_sem.at[0],
+            device_id={"rows": row(1, 0)},
+            device_id_type=MESH,
+        ).wait_send()
 
     def copy(axis, side, item, there):
         kind, dx, dz = item
@@ -166,7 +189,7 @@
         return pltpu.make_async_remote_copy(
             src_ref=ref,
             dst_ref=ref,
-            send_sem=send_sem.at[n],
+            send_sem=send_sem_of(kind),
             recv_sem=recv_sem.at[n],
             device_id={"rows": target},
             device_id_type=MESH,
@@ -184,7 +207,7 @@
         return pltpu.make_async_remote_copy(
             src_ref=ref,
             dst_ref=ref,
-            send_sem=send_sem.at[n],
+            send_sem=send_sem_of(kind),
             recv_sem=recv_sem.at[n],
             device_id={"rows": row(1, 0)},
             device_id_type=MESH,
@@ -203,13 +226,27 @@
         else:
             oq[cut:, lanes] = flat.T
 
-    sent, swap = [], None
+    def join_norm():
+        g = [sums[i].reshape(Z * X // 2, 2, 128) for i in range(2)]
+        parts = [g[j % 2][:, j // 2] for j in range(4)]
+        total = parts[0]
+        for j in range(1, 4):
+            total = total + pltpu.roll(parts[j], 32 * j, axis=1)
+        on[...] = total.astype(jnp.bfloat16)
+
+    swap, late = None, len(steps) - 16
+    ready = {1}
     here = {(kind, dz): {0} if dz == 0 else set() for kind in range(len(PIECES)) for dz in range(Z)}
-    for step in steps:
+    for at, step in enumerate(steps):
+        if at == late:
+            swap.wait()
+            join_norm()
         if step[0] == "send":
-            c = copy(*step[1:])
-            c.start()
-            sent.append(c)
+            kind, dx, dz = step[3]
+            if kind in (0, 2) and kind not in ready and (dx, dz) == (0, 0):
+                merge_query()
+                ready = {0, 1, 2}
+            copy(*step[1:]).start()
         elif step[0] == "swap":
             swap = pltpu.make_async_remote_copy(
                 src_ref=sums.at[tp],
@@ -235,15 +272,8 @@
                 turn(kind, zz * 2 + mx // 2)
             if after[1] and not before[1]:
                 turn(kind, zz * 2 + 1 - mx // 2)
-    swap.wait()
-    g = [sums[i].reshape(Z * X // 2, 2, 128) for i in range(2)]
-    parts = [g[j % 2][:, j // 2] for j in range(4)]
-    total = parts[0]
-    for j in range(1, 4):
-        total = total + pltpu.roll(parts[j], 32 * j, axis=1)
-    on[...] = total.astype(jnp.bfloat16)
-    for c in sent:
-        c.wait_send()
+    for kind in ("sum_x", "sum_z", *range(len(PIECES))):
+        all_sent(kind)
 
 
 def write_out(*refs):
@@ -280,7 +310,7 @@
             *(pltpu.VMEM((n, rows, columns), jnp.bfloat16) for _, columns, _ in PIECES),
             pltpu.VMEM((2, n, 1, 128), jnp.float32),
             pltpu.SemaphoreType.DMA((11,)),
-            pltpu.SemaphoreType.DMA((len(places),)),
+            pltpu.SemaphoreType.DMA((len(PIECES) + 2,)),
             pltpu.SemaphoreType.DMA((len(places),)),
             pltpu.SemaphoreType.DMA((2,)),
         ],

time: 54.1 us -> 53.2 us (0.983)
  Pallas kernels: 53.3 us -> 52.5 us
    pallas_call x1, Pallas kernels: 50.6 us -> 49.8 us  [local(): pl.pallas_call(functools.partial(kernel, steps, places), name='gather', o...]
where the time goes in v3:
time: 53.2 us; the launch traced here: 53.1 us
  Pallas kernels  52.5 us (99%)
  between operations  0.64 us (1%)
    pallas_call x1, Pallas kernels, local(): pl.pallas_call(functools.partial(kernel, steps, places), name='gather', o...  49.8 us
    pallas_call x1, Pallas kernels, local(): pl.pallas_call(write_out, name='write', out_shape=tuple((jax.ShapeDtypeSt...  2.71 us

profile of v3, /device:TPU:56, one launch (start us, length us, event | category | flops | bytes accessed | tf_op | source)
XLA Modules:
  0.0 53.1 jit_solution(1399853713950384985)
XLA Ops:
  0.6 49.8 %gather.1 = (bf16[1024,2048]{1,0:T(8,128)(2,1)S(1)}, bf16[256,2048]{1,0:T(8,128)(2,1)S(1)}, bf16[256,2048]{1,0:T(8,128)(2,1)S(1)}, bf16[16,128]{1,0:T(8,128)(2,1)S(1)}) custom-call(bf16[64,1024]{1,0:T(8,128)(2,1)} %tq.1, bf16[16,64]{1,0:T(8,128)(2,1)} %bitcast.6, bf16[16,1024]{1,0:T(8,128)(2,1)} %hq.1, bf16[64,256]{1,0:T(8,128)(2,1)} %tk.1, ...), custom_call_target="tpu_custom_call" | custom-call | tf_op jit(solution)/shard_map/gather/pallas_call | solution.py:297
  50.4 2.7 %write.1 = (bf16[1024,2048]{1,0:T(8,128)(2,1)}, bf16[256,2048]{1,0:T(8,128)(2,1)}, bf16[256,2048]{1,0:T(8,128)(2,1)}, bf16[16,128]{1,0:T(8,128)(2,1)}) custom-call(bf16[1024,2048]{1,0:T(8,128)(2,1)S(1)} %get-tuple-element.12.refs_0_, bf16[256,2048]{1,0:T(8,128)(2,1)S(1)} %get-tuple-element.13.refs_1_, bf16[256,2048]{1,0:T(8,128)(2,1)S(1)} %get-tuple-element.14.refs_2_, ...), custom_call_target="tpu_custom_call" | custom-call | tf_op jit(solution)/shard_map/write/pallas_call | solution.py:322

commit v4 on v3

--- a/solution.py
+++ b/solution.py
@@ -15,10 +15,14 @@
 Z, X = 8, 4
 RATE = 46650.0
 HOP = 2.0
-DEPTH = 2
-
-PIECES = (("x", 640, 1), ("z", 512, 1), ("z", 384, -1))
-FIRST = (1, 0, 2)
+DEPTH = 3
+
+MEET = 8
+
+PIECES = (("z", 512, -1), ("x", 384, 1), ("x", 256, -1), ("z", 384, 1))
+SPANS = (((1, 0, 256), (2, 0, 256)), ((0, 0, 384),), ((0, 384, 640),), ((0, 640, 1024),))
+FIRST = (0, 1, 2, 3)
+UP = ((0, 1), (2, 1), (1, 2))
 
 
 def onward(d, size, far):
@@ -40,7 +44,7 @@
     if axis == "x":
         if dz == 0:
             out += [("x", s, (kind, n, 0)) for n, s in onward(dx, X, far)]
-        out += [("z", s, (kind, dx, n)) for n, s in onward(dz, Z, 1 if dx % 2 == 0 else -1)]
+        out += [("z", s, (kind, dx, n)) for n, s in onward(dz, Z, 1 if (dx % X, kind) in UP else -1)]
     else:
         if dx == 0:
             out += [("z", s, (kind, 0, n)) for n, s in onward(dz, Z, far)]
@@ -57,10 +61,10 @@
     links = {(a, s): [] for a in "xz" for s in (1, -1)}
     given = {k: [] for k in links}
     events, tick, steps = [], itertools.count(), []
-    norm_x, norm_z = 1, 1
+    norm_x, norm_z, waits = 1, 1, 0
 
     def cost(item):
-        return (512 if isinstance(item[0], str) else PIECES[item[0]][1] * 128) / RATE
+        return (1024 if isinstance(item[0], str) else PIECES[item[0]][1] * 128) / RATE
 
     def offer(item):
         for axis, side, there in forwards(item):
@@ -81,7 +85,6 @@
                 if len(given[k]) == 1:
                     begin(k, now)
 
-    offer(("sum_x", 0, 0))
     for kind in FIRST:
         offer((kind, 0, 0))
     feed(0.0)
@@ -95,6 +98,10 @@
             feed(now)
             continue
         steps.append(("wait", item))
+        waits += 1
+        if waits == MEET:
+            steps.append(("meet",))
+            offer(("sum_x", 0, 0))
         if item[0] == "sum_x":
             norm_x += 1
             if norm_x == X:
@@ -104,7 +111,7 @@
         offer(item)
         feed(now)
         if item[0] == "sum_z" and norm_z == Z:
-            steps.append(("swap",))
+            steps.append(("join",))
     return steps
 
 
@@ -112,7 +119,7 @@
     steps, places, tq, lq, hq, tk, lk, hk, tv, lv, hv, nt, ns, oq, ok, ov, on, *scratch
 ):
     vin, blocks, sums = scratch[:11], scratch[11 : 11 + len(PIECES)], scratch[11 + len(PIECES)]
-    in_sem, send_sem, recv_sem, swap_sem = scratch[12 + len(PIECES) :]
+    in_sem, send_sem, recv_sem, pair_sem = scratch[12 + len(PIECES) :]
     me, tp = lax.axis_index("rows"), lax.axis_index("tp")
     mz, mx = me // X, me % X
 
@@ -122,7 +129,11 @@
     barrier = pltpu.get_barrier_semaphore()
     for there in (row(1, 0), row(-1, 0), row(0, 1), row(0, -1)):
         pl.semaphore_signal(barrier, inc=1, device_id={"rows": there}, device_id_type=MESH)
-    pl.semaphore_signal(barrier, inc=1, device_id={"tp": 1 - tp}, device_id_type=MESH)
+
+    @pl.when(tp == 0)
+    def _():
+        pl.semaphore_signal(barrier, inc=1, device_id={"tp": 1}, device_id_type=MESH)
+
 
     loads = [
         pltpu.make_async_copy(a, b, in_sem.at[i])
@@ -140,21 +151,40 @@
         )
         return (train[:, lo:hi].astype(jnp.float32) + mix_rate * product).astype(jnp.bfloat16)
 
-    cut = PIECES[0][1]
-    width = vtq.shape[1]
-    kv = vtk.shape[1]
-    sums[tp, me] = jnp.concatenate(
-        [vnt[...] + vns[...], jnp.zeros((1, 128 - vnt.shape[1]), jnp.float32)], axis=1
-    )
-    blocks[1][me, :, :kv] = merged(vtk, vlk, vhk, 0, kv)
-    blocks[1][me, :, kv:] = merged(vtv, vlv, vhv, 0, kv)
-    pl.semaphore_wait(barrier, 5)
+    sources = ((vtq, vlq, vhq), (vtk, vlk, vhk), (vtv, vlv, vhv))
+    outs = (oq, ok, ov)
+
+    def merge(kind):
+        at = 0
+        for array, lo, hi in SPANS[kind]:
+            blocks[kind][me, :, at : at + hi - lo] = merged(*sources[array], lo, hi)
+            at += hi - lo
 
     def merge_query():
         for load in loads[:3]:
             load.wait()
-        blocks[0][me] = merged(vtq, vlq, vhq, 0, cut)
-        blocks[2][me] = merged(vtq, vlq, vhq, cut, width)
+        for kind in range(1, len(PIECES)):
+            merge(kind)
+
+    sums[me, tp] = jnp.concatenate(
+        [vnt[...] + vns[...], jnp.zeros((1, 128 - vnt.shape[1]), jnp.float32)], axis=1
+    )
+    merge(0)
+    pl.semaphore_wait(barrier, 4 + tp)
+
+    def pair_copy(core):
+        return pltpu.make_async_remote_copy(
+            src_ref=sums.at[me, core],
+            dst_ref=sums.at[me, core],
+            send_sem=pair_sem.at[0],
+            recv_sem=pair_sem.at[1],
+            device_id={"tp": 1 - tp},
+            device_id_type=MESH,
+        )
+
+    @pl.when(tp == 1)
+    def _():
+        pair_copy(1).start()
 
     def send_sem_of(kind):
         return send_sem.at[("sum_x", "sum_z").index(kind) + len(PIECES) if isinstance(kind, str) else kind]
@@ -162,9 +192,9 @@
     def all_sent(kind):
         count = Z * X - 1
         if kind == "sum_x":
-            ref = sums.at[tp, pl.ds(0, X - 1)]
+            ref = sums.at[pl.ds(0, X - 1)]
         elif kind == "sum_z":
-            ref = sums.at[tp, pl.ds(0, (Z - 1) * X)]
+            ref = sums.at[pl.ds(0, (Z - 1) * X)]
         else:
             ref = blocks[kind].at[pl.ds(0, count)]
         pltpu.make_async_remote_copy(
@@ -179,9 +209,9 @@
     def copy(axis, side, item, there):
         kind, dx, dz = item
         if kind == "sum_x":
-            ref = sums.at[tp, row(dx, 0)]
+            ref = sums.at[row(dx, 0)]
         elif kind == "sum_z":
-            ref = sums.at[tp, pl.ds(((mz - dz + Z) % Z) * X, X)]
+            ref = sums.at[pl.ds(((mz - dz + Z) % Z) * X, X)]
         else:
             ref = blocks[kind].at[row(dx, dz)]
         target = row(-side, 0) if axis == "x" else row(0, -side)
@@ -198,9 +228,9 @@
     def landed(item):
         kind, dx, dz = item
         if kind == "sum_x":
-            ref = sums.at[tp, row(dx, 0)]
+            ref = sums.at[row(dx, 0)]
         elif kind == "sum_z":
-            ref = sums.at[tp, pl.ds(((mz - dz + Z) % Z) * X, X)]
+            ref = sums.at[pl.ds(((mz - dz + Z) % Z) * X, X)]
         else:
             ref = blocks[kind].at[row(dx, dz)]
         n = places[item]
@@ -218,45 +248,40 @@
         rows, columns = both.shape[1], both.shape[2]
         lanes = pl.ds(pl.multiple_of(pair * 2 * rows, 2 * rows), 2 * rows)
         flat = both.reshape(2 * rows, columns)
-        if kind == 0:
-            oq[:columns, lanes] = flat.T
-        elif kind == 1:
-            ok[:, lanes] = flat[:, :kv].T
-            ov[:, lanes] = flat[:, kv:].T
-        else:
-            oq[cut:, lanes] = flat.T
+        at = 0
+        for array, lo, hi in SPANS[kind]:
+            outs[array][lo:hi, lanes] = flat[:, at : at + hi - lo].T
+            at += hi - lo
 
     def join_norm():
-        g = [sums[i].reshape(Z * X // 2, 2, 128) for i in range(2)]
-        parts = [g[j % 2][:, j // 2] for j in range(4)]
-        total = parts[0]
+        parts = sums[...].reshape(Z * X // 2, 4, 128)
+        total = parts[:, 0]
         for j in range(1, 4):
-            total = total + pltpu.roll(parts[j], 32 * j, axis=1)
+            total = total + pltpu.roll(parts[:, j], 32 * j, axis=1)
         on[...] = total.astype(jnp.bfloat16)
 
-    swap, late = None, len(steps) - 16
-    ready = {1}
+    merged_all = False
     here = {(kind, dz): {0} if dz == 0 else set() for kind in range(len(PIECES)) for dz in range(Z)}
-    for at, step in enumerate(steps):
-        if at == late:
-            swap.wait()
-            join_norm()
+    for step in steps:
         if step[0] == "send":
             kind, dx, dz = step[3]
-            if kind in (0, 2) and kind not in ready and (dx, dz) == (0, 0):
+            if not (merged_all or isinstance(kind, str) or kind == 0):
                 merge_query()
-                ready = {0, 1, 2}
+                merged_all = True
             copy(*step[1:]).start()
-        elif step[0] == "swap":
-            swap = pltpu.make_async_remote_copy(
-                src_ref=sums.at[tp],
-                dst_ref=sums.at[tp],
-                send_sem=swap_sem.at[0],
-                recv_sem=swap_sem.at[1],
-                device_id={"tp": 1 - tp},
-                device_id_type=MESH,
-            )
-            swap.start()
+        elif step[0] == "meet":
+
+            @pl.when(tp == 0)
+            def _():
+                pair_copy(1).wait_recv()
+                pair_copy(0).start()
+
+            @pl.when(tp == 1)
+            def _():
+                pair_copy(0).wait_recv()
+
+        elif step[0] == "join":
+            join_norm()
         else:
             item = step[1]
             landed(item).wait_recv()
@@ -274,6 +299,7 @@
                 turn(kind, zz * 2 + 1 - mx // 2)
     for kind in ("sum_x", "sum_z", *range(len(PIECES))):
         all_sent(kind)
+    pair_copy(tp).wait_send()
 
 
 def write_out(*refs):
@@ -308,7 +334,7 @@
         scratch_shapes=[
             *(pltpu.VMEM(a.shape, a.dtype) for a in args),
             *(pltpu.VMEM((n, rows, columns), jnp.bfloat16) for _, columns, _ in PIECES),
-            pltpu.VMEM((2, n, 1, 128), jnp.float32),
+            pltpu.VMEM((n, 2, 1, 128), jnp.float32),
             pltpu.SemaphoreType.DMA((11,)),
             pltpu.SemaphoreType.DMA((len(PIECES) + 2,)),
             pltpu.SemaphoreType.DMA((len(places),)),

time: 53.2 us -> 51.2 us (0.962)
  Pallas kernels: 52.5 us -> 50.3 us
    pallas_call x1, Pallas kernels: 49.8 us -> 47.6 us  [local(): pl.pallas_call(functools.partial(kernel, steps, places), name='gather', o...]
where the time goes in v4:
time: 51.2 us; the launch traced here: 50.9 us
  Pallas kernels  50.3 us (98%)
  between operations  0.64 us (1%)
    pallas_call x1, Pallas kernels, local(): pl.pallas_call(functools.partial(kernel, steps, places), name='gather', o...  47.6 us
    pallas_call x1, Pallas kernels, local(): pl.pallas_call(write_out, name='write', out_shape=tuple((jax.ShapeDtypeSt...  2.71 us

profile of v4, /device:TPU:56, one launch (start us, length us, event | category | flops | bytes accessed | tf_op | source)
XLA Modules:
  0.0 50.9 jit_solution(9084235371069976644)
XLA Ops:
  0.6 47.6 %gather.1 = (bf16[1024,2048]{1,0:T(8,128)(2,1)S(1)}, bf16[256,2048]{1,0:T(8,128)(2,1)S(1)}, bf16[256,2048]{1,0:T(8,128)(2,1)S(1)}, bf16[16,128]{1,0:T(8,128)(2,1)S(1)}) custom-call(bf16[64,1024]{1,0:T(8,128)(2,1)} %tq.1, bf16[16,64]{1,0:T(8,128)(2,1)} %bitcast.6, bf16[16,1024]{1,0:T(8,128)(2,1)} %hq.1, bf16[64,256]{1,0:T(8,128)(2,1)} %tk.1, ...), custom_call_target="tpu_custom_call" | custom-call | tf_op jit(solution)/shard_map/gather/pallas_call | solution.py:323
  48.2 2.7 %write.1 = (bf16[1024,2048]{1,0:T(8,128)(2,1)}, bf16[256,2048]{1,0:T(8,128)(2,1)}, bf16[256,2048]{1,0:T(8,128)(2,1)}, bf16[16,128]{1,0:T(8,128)(2,1)}) custom-call(bf16[1024,2048]{1,0:T(8,128)(2,1)S(1)} %get-tuple-element.12.refs_0_, bf16[256,2048]{1,0:T(8,128)(2,1)S(1)} %get-tuple-element.13.refs_1_, bf16[256,2048]{1,0:T(8,128)(2,1)S(1)} %get-tuple-element.14.refs_2_, ...), custom_call_target="tpu_custom_call" | custom-call | tf_op jit(solution)/shard_map/write/pallas_call | solution.py:348

commit v5 on v4

--- a/solution.py
+++ b/solution.py
@@ -260,7 +260,7 @@
             total = total + pltpu.roll(parts[:, j], 32 * j, axis=1)
         on[...] = total.astype(jnp.bfloat16)
 
-    merged_all = False
+    merged_all, later = False, []
     here = {(kind, dz): {0} if dz == 0 else set() for kind in range(len(PIECES)) for dz in range(Z)}
     for step in steps:
         if step[0] == "send":
@@ -283,6 +283,9 @@
         elif step[0] == "join":
             join_norm()
         else:
+            for block in later:
+                turn(*block)
+            later = []
             item = step[1]
             landed(item).wait_recv()
             kind, dx, dz = item
@@ -294,9 +297,11 @@
             after = {0, 1, 3} <= got, len(got) == X
             zz = (mz - dz + Z) % Z
             if after[0] and not before[0]:
-                turn(kind, zz * 2 + mx // 2)
+                later.append((kind, zz * 2 + mx // 2))
             if after[1] and not before[1]:
-                turn(kind, zz * 2 + 1 - mx // 2)
+                later.append((kind, zz * 2 + 1 - mx // 2))
+    for block in later:
+        turn(*block)
     for kind in ("sum_x", "sum_z", *range(len(PIECES))):
         all_sent(kind)
     pair_copy(tp).wait_send()

time: 51.2 us -> 51.4 us (level)
  no operation moved by 1% of the time
where the time goes in v5:
time: 51.4 us; the launch traced here: 50.9 us
  Pallas kernels  50.3 us (98%)
  between operations  0.64 us (1%)
    pallas_call x1, Pallas kernels, local(): pl.pallas_call(functools.partial(kernel, steps, places), name='gather', o...  47.6 us
    pallas_call x1, Pallas kernels, local(): pl.pallas_call(write_out, name='write', out_shape=tuple((jax.ShapeDtypeSt...  2.71 us

profile of v5, /device:TPU:56, one launch (start us, length us, event | category | flops | bytes accessed | tf_op | source)
XLA Modules:
  0.0 50.9 jit_solution(16752116933317337116)
XLA Ops:
  0.6 47.6 %gather.1 = (bf16[1024,2048]{1,0:T(8,128)(2,1)S(1)}, bf16[256,2048]{1,0:T(8,128)(2,1)S(1)}, bf16[256,2048]{1,0:T(8,128)(2,1)S(1)}, bf16[16,128]{1,0:T(8,128)(2,1)S(1)}) custom-call(bf16[64,1024]{1,0:T(8,128)(2,1)} %tq.1, bf16[16,64]{1,0:T(8,128)(2,1)} %bitcast.6, bf16[16,1024]{1,0:T(8,128)(2,1)} %hq.1, bf16[64,256]{1,0:T(8,128)(2,1)} %tk.1, ...), custom_call_target="tpu_custom_call" | custom-call | tf_op jit(solution)/shard_map/gather/pallas_call | solution.py:328
  48.2 2.7 %write.1 = (bf16[1024,2048]{1,0:T(8,128)(2,1)}, bf16[256,2048]{1,0:T(8,128)(2,1)}, bf16[256,2048]{1,0:T(8,128)(2,1)}, bf16[16,128]{1,0:T(8,128)(2,1)}) custom-call(bf16[1024,2048]{1,0:T(8,128)(2,1)S(1)} %get-tuple-element.12.refs_0_, bf16[256,2048]{1,0:T(8,128)(2,1)S(1)} %get-tuple-element.13.refs_1_, bf16[256,2048]{1,0:T(8,128)(2,1)S(1)} %get-tuple-element.14.refs_2_, ...), custom_call_target="tpu_custom_call" | custom-call | tf_op jit(solution)/shard_map/write/pallas_call | solution.py:353
